TPU v7x, 32 devices: a whole 2x2x4 slice. The times are simulated.
32 devices in a mesh: dp: 16 (over z, y, core), tensor: 2 (over x).
Axes of the slice: x: 2, y: 2, z: 4, core: 2. Of those that a mesh axis runs over, the one named last changes fastest.
Arguments:
- step: int32 [1], replicated, may hold values from 0 to 999
- activations: bfloat16 [2, 16384, 8192], P(None, 'dp', 'tensor'), may hold values from -6 to 6
- grad_weight: bfloat16 [2, 8192, 28672], P(None, 'tensor', 'dp'), may hold values from -6 to 6
Outputs:
- preconditioned: float32 [8192, 28672], P('tensor', 'dp')
All inputs are finite; a program needn't handle non-finite values.
Results may differ from a plain program's by a relative error of at most 0.0044.
Values may be sent and summed in bfloat16 or wider, within the bound.
No kernel may reach another device: no remote copies, remote signals or barrier semaphores. Data moves between devices by JAX's collectives and lax.ppermute only.
A program may use at most 192 MiB of HBM per device.

v0:
```python
import jax
import jax.numpy as jnp
from jax import lax
from jax.sharding import PartitionSpec as P

BLOCK = 1024
LAYERS = 2
ITERS = 4


def local(step, activations, grad_weight):
    groups = lax.axis_size("dp")
    layer = step[0] % LAYERS
    damping = 0.05 + 0.1 * step[0].astype(jnp.float32) / 1000.0
    acts = lax.dynamic_index_in_dim(activations, layer, 0, keepdims=False)
    grads = lax.dynamic_index_in_dim(grad_weight, layer, 0, keepdims=False)
    tok_rows = acts.shape[0]
    width = acts.shape[1]
    nblock = width // BLOCK
    share = BLOCK // groups
    blocks = acts.reshape(tok_rows, nblock, BLOCK)
    total_tokens = tok_rows * groups
    first = lax.axis_index("dp") * share
    summed = lax.psum(
        jnp.einsum("tkr,tkc->rkc", blocks, blocks, preferred_element_type=jnp.float32), "dp"
    )
    gram_rows = lax.dynamic_slice_in_dim(summed, first, share, 0)
    row_ids = first + lax.broadcasted_iota(jnp.int32, (share, 1, BLOCK), 0)
    col_ids = lax.broadcasted_iota(jnp.int32, (share, 1, BLOCK), 2)
    identity = (row_ids == col_ids).astype(jnp.float32)
    factor = gram_rows / total_tokens + damping * identity
    block_squares = lax.psum(jnp.sum(factor * factor, axis=(0, 2)), "dp")
    largest = lax.pmax(jnp.max(block_squares), "tensor")
    iterate = jnp.broadcast_to(identity / jnp.sqrt(largest), factor.shape)
    for sweep in range(ITERS):
        whole = lax.all_gather(iterate, "dp", axis=0, tiled=True)
        product = jnp.einsum("rkj,jkc->rkc", factor, whole, precision=lax.Precision.HIGHEST)
        iterate = 2.0 * iterate - jnp.einsum(
            "rkj,jkc->rkc", product, whole, precision=lax.Precision.HIGHEST
        )
    inverse = iterate.astype(jnp.bfloat16)
    stacked = grads.reshape(nblock, BLOCK, grads.shape[1])
    result = jnp.einsum(
        "rkc,kcf->krf",
        lax.all_gather(inverse, "dp", axis=0, tiled=True),
        stacked,
        preferred_element_type=jnp.float32,
    )
    return result.reshape(width, grads.shape[1])


def solution(mesh):
    in_specs = (P(), P(None, "dp", "tensor"), P(None, "tensor", "dp"))
    out_specs = P("tensor", "dp")
    return jax.shard_map(local, mesh=mesh, in_specs=in_specs, out_specs=out_specs, check_vma=False)
```

profile of v0, /device:TPU:0, one launch (start us, length us, event | category | flops | bytes accessed | tf_op | source)
XLA Modules:
  0.0 1019.5 jit_solution(3891566731821359104)
XLA Ops:
  7.2 7.9 constant_dynamic-slice_fusion.1
  15.1 12.0 %copy.23 = bf16[1,1024,4096]{1,2,0:T(8,128)(2,1)} copy(bf16[1,1024,4096]{2,1,0:T(8,128)(2,1)} %constant_dynamic-slice_fusion.1) | data formatting | bytes 16777216
  27.1 17.1 %convolution_bitcast_fusion = f32[1024,4,1024]{2,0,1:T(8,128)} fusion(bf16[1024,4,1024]{0,2,1:T(8,128)(2,1)} %bitcast.51), kind=kOutput, calls=%fused_computation | convolution fusion | flops 8589934592 | bytes 25165824 | tf_op jit(solution)/shard_map/tkr,tkc->rkc/dot_general | solution.py:25
  44.4 300.7 %all-reduce.2.cloned.1.call-done = f32[1024,4,1024]{2,0,1:T(8,128)} async-done(((f32[1024,4,1024]{2,0,1:T(8,128)}), f32[1024,4,1024]{2,0,1:T(8,128)}) %all-reduce.2.cloned.1.call-update) | async-done | bytes 16777232 | tf_op jit(solution)/shard_map/psum | solution.py:24
  345.1 1.5 multiply_reduce_fusion
  346.6 31.8 %psum.15 = f32[4]{0:T(128)S(1)} all-reduce(f32[4]{0:T(128)S(1)} %multiply_reduce_fusion), channel_id=1, replica_groups=mesh['dp'=16,'tensor'=2] {'dp'}, use_global_device_ids=true, to_apply=%region_2.3 | all-reduce | flops 4 | bytes 32 | tf_op jit(solution)/shard_map/psum | solution.py:32
  378.4 0.6 reduce_max.9
  379.0 5.5 pmax.7
  385.2 0.8 broadcast_multiply_fusion
  386.3 47.5 %all-gather.14.cloned.1.call-done = f32[1024,1024]{1,0:T(8,128)} async-done(((f32[64,1024]{1,0:T(8,128)}), f32[1024,1024]{1,0:T(8,128)}) %all-gather.14.cloned.1.call-update) | async-done | bytes 4194320 | tf_op jit(solution)/shard_map/all_gather | solution.py:36
  433.8 11.8 %fusion.4 = f32[64,4,1024]{2,0,1:T(8,128)S(1)} fusion(f32[1024,1024]{1,0:T(8,128)} %all-gather.14.cloned.1.call-done, f32[1024,4,1024]{2,0,1:T(8,128)} %all-reduce.2.cloned.1.call-done, s32[]{:T(128)S(6)} %select_n.18, f32[64,1024]{1,0:T(8,128)S(1)} %fusion.18), kind=kOutput, calls=%fused_computation.5 | convolution fusion | flops 3221749760 | bytes 6553604 | tf_op jit(solution)/shard_map/rkj,jkc->rkc/dot_general | solution.py:37
  445.6 12.8 %fusion.10 = f32[64,4,1024]{2,0,1:T(8,128)} fusion(f32[64,4,1024]{2,0,1:T(8,128)S(1)} %fusion.4, f32[1024,1024]{1,0:T(8,128)} %all-gather.14.cloned.1.call-done, f32[64,1024]{1,0:T(8,128)S(1)} %get-tuple-element.5), kind=kOutput, calls=%fused_computation.7 | convolution fusion | flops 3221487616 | bytes 6553600 | tf_op jit(solution)/shard_map/rkj,jkc->rkc/dot_general | solution.py:38
  458.4 125.1 %all-gather.6.cloned.1.call-done = f32[1024,4,1024]{2,0,1:T(8,128)} async-done(((f32[64,4,1024]{2,0,1:T(8,128)}), f32[1024,4,1024]{2,0,1:T(8,128)}) %all-gather.6.cloned.1.call-update) | async-done | bytes 16777232 | tf_op jit(solution)/shard_map/all_gather | solution.py:36
  583.5 15.3 %convolution_bitcast_fusion.6 = f32[64,4,1024]{2,0,1:T(8,128)S(1)} fusion(f32[1024,4,1024]{2,0,1:T(8,128)} %all-gather.6.cloned.1.call-done, f32[1024,4,1024]{2,0,1:T(8,128)} %all-reduce.2.cloned.1.call-done, s32[]{:T(128)S(6)} %select_n.18, f32[64,1024]{1,0:T(8,128)S(1)} %fusion.18), kind=kOutput, calls=%fused_computation.16 | convolution fusion | flops 3221749760 | bytes 19136516 | tf_op jit(solution)/shard_map/rkj,jkc->rkc/dot_general | solution.py:37
  598.8 11.8 %fusion.15 = f32[64,4,1024]{2,0,1:T(8,128)} fusion(f32[1024,4,1024]{2,0,1:T(8,128)S(1)} %copy-done.1, f32[64,4,1024]{2,0,1:T(8,128)S(1)} %convolution_bitcast_fusion.6, f32[64,4,1024]{2,0,1:T(8,128)S(1)} %copy-done.4), kind=kOutput, calls=%fused_computation.15 | convolution fusion | flops 3221749760 | bytes 19922944 | tf_op jit(solution)/shard_map/rkj,jkc->rkc/dot_general | solution.py:38
  610.7 124.7 %all-gather.8.cloned.1.call-done = f32[1024,4,1024]{2,0,1:T(8,128)} async-done(((f32[64,4,1024]{2,0,1:T(8,128)}), f32[1024,4,1024]{2,0,1:T(8,128)}) %all-gather.8.cloned.1.call-update) | async-done | bytes 16777232 | tf_op jit(solution)/shard_map/all_gather | solution.py:36
  735.4 15.0 %convolution_bitcast_fusion.4 = f32[64,4,1024]{2,0,1:T(8,128)S(1)} fusion(f32[1024,4,1024]{2,0,1:T(8,128)} %all-gather.8.cloned.1.call-done, f32[1024,4,1024]{2,0,1:T(8,128)} %all-reduce.2.cloned.1.call-done, s32[]{:T(128)S(6)} %select_n.18, f32[64,1024]{1,0:T(8,128)S(1)} %fusion.18), kind=kOutput, calls=%fused_computation.13 | convolution fusion | flops 3221749760 | bytes 19136516 | tf_op jit(solution)/shard_map/rkj,jkc->rkc/dot_general | solution.py:37
  750.4 11.8 %fusion.14 = f32[64,4,1024]{2,0,1:T(8,128)} fusion(f32[1024,4,1024]{2,0,1:T(8,128)S(1)} %copy-done.2, f32[64,4,1024]{2,0,1:T(8,128)S(1)} %convolution_bitcast_fusion.4, f32[64,4,1024]{2,0,1:T(8,128)S(1)} %copy-done.5), kind=kOutput, calls=%fused_computation.12 | convolution fusion | flops 3221749760 | bytes 19922944 | tf_op jit(solution)/shard_map/rkj,jkc->rkc/dot_general | solution.py:38
  762.3 124.7 %all-gather.10.cloned.1.call-done = f32[1024,4,1024]{2,0,1:T(8,128)} async-done(((f32[64,4,1024]{2,0,1:T(8,128)}), f32[1024,4,1024]{2,0,1:T(8,128)}) %all-gather.10.cloned.1.call-update) | async-done | bytes 16777232 | tf_op jit(solution)/shard_map/all_gather | solution.py:36
  887.0 15.0 %convolution_bitcast_fusion.2 = f32[64,4,1024]{2,0,1:T(8,128)S(1)} fusion(f32[1024,4,1024]{2,0,1:T(8,128)} %all-gather.10.cloned.1.call-done, f32[1024,4,1024]{2,0,1:T(8,128)} %all-reduce.2.cloned.1.call-done, s32[]{:T(128)S(6)} %select_n.18, f32[64,1024]{1,0:T(8,128)S(1)} %fusion.18), kind=kOutput, calls=%fused_computation.10 | convolution fusion | flops 3221749760 | bytes 19136516 | tf_op jit(solution)/shard_map/rkj,jkc->rkc/dot_general | solution.py:37
  902.0 11.6 %fusion.16 = bf16[64,4,1024]{2,0,1:T(8,128)(2,1)} fusion(f32[1024,4,1024]{2,0,1:T(8,128)S(1)} %copy-done, f32[64,4,1024]{2,0,1:T(8,128)S(1)} %convolution_bitcast_fusion.2, f32[64,4,1024]{2,0,1:T(8,128)S(1)} %copy-done.3), kind=kOutput, calls=%fused_computation.17 | convolution fusion | flops 3222011904 | bytes 19398656 | tf_op jit(solution)/shard_map/rkj,jkc->rkc/dot_general | solution.py:38
  913.7 13.2 %constant_dynamic-slice_fusion = bf16[1,4096,1792]{2,1,0:T(8,128)(2,1)} fusion(bf16[2,4096,1792]{2,1,0:T(8,128)(2,1)} %param.5, s32[]{:T(128)S(6)} %select_n.17), kind=kLoop, calls=%fused_computation.24 | loop fusion | bytes 29360132 | tf_op jit(solution)/shard_map/jit(dynamic_index_in_dim)/dynamic_slice | solution.py:16
  926.9 59.4 %all-gather.12.cloned.1.call-done = bf16[1024,4,1024]{2,0,1:T(8,128)(2,1)} async-done(((bf16[64,4,1024]{2,0,1:T(8,128)(2,1)}), bf16[1024,4,1024]{2,0,1:T(8,128)(2,1)}) %all-gather.12.cloned.1.call-update) | async-done | bytes 8388624 | tf_op jit(solution)/shard_map/all_gather | solution.py:45
  986.3 25.9 %fusion.19 = f32[4,1024,1792]{2,1,0:T(8,128)} fusion(bf16[1024,4,1024]{2,0,1:T(8,128)(2,1)} %all-gather.12.cloned.1.call-done, bf16[4,1024,1792]{2,1,0:T(8,128)(2,1)} %bitcast.50), kind=kOutput, calls=%fused_computation.27 | convolution fusion | flops 15032385536 | bytes 52428800 | tf_op jit(solution)/shard_map/rkc,kcf->krf/dot_general | solution.py:43
  (26 shorter events, 0.6 us)
Async XLA Ops:
  6.5 338.6 %all-reduce.2.cloned.1.call-start = ((), (), s32[]{:S(2)}) async-start(), calls=%async_computation | async-start | bytes 33554432 | tf_op jit(solution)/shard_map/psum | solution.py:24
  44.3 389.5 %all-gather.14.cloned.1.call-start = ((), (), s32[]{:S(2)}) async-start(), calls=%async_computation.5 | async-start | bytes 4456448 | tf_op jit(solution)/shard_map/all_gather | solution.py:36
  386.0 197.5 %all-gather.6.cloned.1.call-start = ((), (), s32[]{:S(2)}) async-start(), calls=%async_computation.1 | async-start | bytes 17825792 | tf_op jit(solution)/shard_map/all_gather | solution.py:36
  458.3 140.4 %copy-start.4 = (f32[64,4,1024]{2,0,1:T(8,128)S(1)}, f32[64,4,1024]{2,0,1:T(8,128)}, u32[]{:S(2)}) copy-start(f32[64,4,1024]{2,0,1:T(8,128)} %fusion.10) | copy-start | bytes 3145732
  458.4 277.0 %all-gather.8.cloned.1.call-start = ((), (), s32[]{:S(2)}) async-start(), calls=%async_computation.2 | async-start | bytes 17825792 | tf_op jit(solution)/shard_map/all_gather | solution.py:36
  583.5 15.3 %copy-start.1 = (f32[1024,4,1024]{2,0,1:T(8,128)S(1)}, f32[1024,4,1024]{2,0,1:T(8,128)}, u32[]{:S(2)}) copy-start(f32[1024,4,1024]{2,0,1:T(8,128)} %all-gather.6.cloned.1.call-done) | copy-start | bytes 50331652
  610.6 139.8 %copy-start.5 = (f32[64,4,1024]{2,0,1:T(8,128)S(1)}, f32[64,4,1024]{2,0,1:T(8,128)}, u32[]{:S(2)}) copy-start(f32[64,4,1024]{2,0,1:T(8,128)} %fusion.15) | copy-start | bytes 3145732
  610.6 276.4 %all-gather.10.cloned.1.call-start = ((), (), s32[]{:S(2)}) async-start(), calls=%async_computation.3 | async-start | bytes 17825792 | tf_op jit(solution)/shard_map/all_gather | solution.py:36
  735.4 15.0 %copy-start.2 = (f32[1024,4,1024]{2,0,1:T(8,128)S(1)}, f32[1024,4,1024]{2,0,1:T(8,128)}, u32[]{:S(2)}) copy-start(f32[1024,4,1024]{2,0,1:T(8,128)} %all-gather.8.cloned.1.call-done) | copy-start | bytes 50331652
  762.2 139.8 %copy-start.3 = (f32[64,4,1024]{2,0,1:T(8,128)S(1)}, f32[64,4,1024]{2,0,1:T(8,128)}, u32[]{:S(2)}) copy-start(f32[64,4,1024]{2,0,1:T(8,128)} %fusion.14) | copy-start | bytes 3145732
  762.2 224.1 %all-gather.12.cloned.1.call-start = ((), (), s32[]{:S(2)}) async-start(), calls=%async_computation.4 | async-start | bytes 8912896 | tf_op jit(solution)/shard_map/all_gather | solution.py:45
  887.0 15.0 %copy-start = (f32[1024,4,1024]{2,0,1:T(8,128)S(1)}, f32[1024,4,1024]{2,0,1:T(8,128)}, u32[]{:S(2)}) copy-start(f32[1024,4,1024]{2,0,1:T(8,128)} %all-gather.10.cloned.1.call-done) | copy-start | bytes 50331652
Sparse Core Ops, SparseCore 0:
  44.4 300.6 all-reduce.1
  386.1 47.5 all-gather.13
  458.5 124.9 all-gather.5
  610.7 124.6 all-gather.7
  762.3 124.6 all-gather.9
  913.8 72.4 all-gather.11
where the time goes:
time: 1020 us
  waiting for transfers between devices  782 us (77%)
  matrix products  148 us (15%)
  blocking collectives  37.3 us (4%)
  local copies, waits for them, and re-layouts  33.2 us (3%)
  between operations  15.4 us (2%)
    all_gather x4, waiting for transfers between devices, local(): whole = lax.all_gather(iterate, 'dp', axis=0, tiled=True)  422 us
    psum x1, waiting for transfers between devices, local(): lax.psum(jnp.einsum('tkr,tkc->rkc', blocks, blocks, preferred_element_typ...  301 us
    all_gather x1, waiting for transfers between devices, local(): lax.all_gather(inverse, 'dp', axis=0, tiled=True)  59.4 us
    dot_general x4, matrix products, local(): jnp.einsum('rkj,jkc->rkc', factor, whole, precision=lax.Precision.HIGHEST)  57 us
    dot_general x4, matrix products, local(): jnp.einsum('rkj,jkc->rkc', product, whole, precision=lax.Precision.HIGHEST)  48 us
    psum x1, blocking collectives, local(): block_squares = lax.psum(jnp.sum(factor * factor, axis=(0, 2)), 'dp')  31.8 us
    dot_general x1, matrix products, local(): jnp.einsum('rkc,kcf->krf', lax.all_gather(inverse, 'dp', axis=0, tiled=Tr...  25.9 us
  transfers between devices with their start and end apart: 6, of which 6 were waited for; matrix products, arithmetic and copies ran while one was open for 1% of the time, Pallas kernels for 0%

commit v1 on v0

--- a/solution.py
+++ b/solution.py
@@ -6,6 +6,30 @@
 BLOCK = 1024
 LAYERS = 2
 ITERS = 4
+
+
+def on_each_block(x, axis, dim, work, out_dim):
+    count, mine, rows = (lax.axis_size(axis), lax.axis_index(axis), x.shape[dim])
+    right = [(i, (i + 1) % count) for i in range(count)]
+    left = [(b, a) for a, b in right]
+    lower, upper = (lax.ppermute(x, axis, right), lax.ppermute(x, axis, left))
+    made = work(x, mine * rows)
+    length = made.shape[out_dim]
+    out = jnp.zeros((*made.shape[:out_dim], count * length, *made.shape[out_dim + 1 :]), made.dtype)
+
+    def put(out, made, owner):
+        return lax.dynamic_update_slice_in_dim(out, made, owner * length, axis=out_dim)
+
+    out = put(out, made, mine)
+    for hop in range(1, count // 2 + 1):
+        below, above = ((mine - hop) % count, (mine + hop) % count)
+        held = (lower, upper)
+        if hop < count // 2:
+            lower, upper = (lax.ppermute(lower, axis, right), lax.ppermute(upper, axis, left))
+        out = put(out, work(held[0], below * rows), below)
+        if 2 * hop < count:
+            out = put(out, work(held[1], above * rows), above)
+    return out
 
 
 def local(step, activations, grad_weight):
@@ -40,11 +64,14 @@
         )
     inverse = iterate.astype(jnp.bfloat16)
     stacked = grads.reshape(nblock, BLOCK, grads.shape[1])
-    result = jnp.einsum(
-        "rkc,kcf->krf",
-        lax.all_gather(inverse, "dp", axis=0, tiled=True),
-        stacked,
-        preferred_element_type=jnp.float32,
+    result = on_each_block(
+        inverse,
+        "dp",
+        0,
+        lambda part, offset: jnp.einsum(
+            "rkc,kcf->krf", part, stacked, preferred_element_type=jnp.float32
+        ),
+        1,
     )
     return result.reshape(width, grads.shape[1])
 

time: 1020 us -> 1050 us (1.029)
  waiting for transfers between devices: 782 us -> 714 us
  matrix products: 148 us -> 193 us
  starting transfers between devices: 0.42 us -> 33.5 us
  local copies, waits for them, and re-layouts: 33.2 us -> 46.2 us
    all_gather x1 -> x0, waiting for transfers between devices: 59.4 us -> none  [local(): lax.all_gather(inverse, 'dp', axis=0, tiled=True)]
    dot_general x1 -> x16, matrix products: 25.9 us -> 71.8 us  [local(): jnp.einsum('rkc,kcf->krf', part, stacked, preferred_element_type=jnp.floa...]
    ppermute x0 -> x15, starting transfers between devices: none -> 33.1 us  [the longest x6 23.5 us: on_each_block(): lax.ppermute(upper, axis, left)]
    all_gather x4, waiting for transfers between devices: 422 us -> 408 us  [local(): whole = lax.all_gather(iterate, 'dp', axis=0, tiled=True)]
    broadcast_in_dim x0 -> x1, local copies, waits for them, and re-layouts: none -> 12.8 us  [on_each_block(): jnp.zeros((*made.shape[:out_dim], count * length, *made.shape[out_dim + 1...]
  transfers between devices with their start and end apart: 6 -> 20, of which waited for: 6 -> 6; matrix products, arithmetic and copies ran while one was open for 1% -> 9% of each run, Pallas kernels for 0% -> 0%
where the time goes in v1:
time: 1050 us; the launch traced here: 1040 us
  waiting for transfers between devices  714 us (68%)
  matrix products  193 us (18%)
  local copies, waits for them, and re-layouts  46.2 us (4%)
  blocking collectives  37.3 us (4%)
  starting transfers between devices  33.5 us (3%)
  between operations  15.5 us (1%)
    all_gather x4, waiting for transfers between devices, local(): whole = lax.all_gather(iterate, 'dp', axis=0, tiled=True)  408 us
    psum x1, waiting for transfers between devices, local(): lax.psum(jnp.einsum('tkr,tkc->rkc', blocks, blocks, preferred_element_typ...  301 us
    dot_general x16, matrix products, local(): jnp.einsum('rkc,kcf->krf', part, stacked, preferred_element_type=jnp.floa...  71.8 us
    dot_general x4, matrix products, local(): jnp.einsum('rkj,jkc->rkc', factor, whole, precision=lax.Precision.HIGHEST)  57.2 us
    dot_general x4, matrix products, local(): jnp.einsum('rkj,jkc->rkc', product, whole, precision=lax.Precision.HIGHEST)  47.2 us
    psum x1, blocking collectives, local(): block_squares = lax.psum(jnp.sum(factor * factor, axis=(0, 2)), 'dp')  31.8 us
    ppermute x6, starting transfers between devices, on_each_block(): lax.ppermute(upper, axis, left)  23.5 us
  transfers between devices with their start and end apart: 20, of which 6 were waited for; matrix products, arithmetic and copies ran while one was open for 9% of the time, Pallas kernels for 0%

profile of v1, /device:TPU:0, one launch (start us, length us, event | category | flops | bytes accessed | tf_op | source)
XLA Modules:
  0.0 1043.3 jit_solution(17649061845706564926)
XLA Ops:
  7.2 7.9 constant_dynamic-slice_fusion.1
  15.1 12.0 %copy.23 = bf16[1,1024,4096]{1,2,0:T(8,128)(2,1)} copy(bf16[1,1024,4096]{2,1,0:T(8,128)(2,1)} %constant_dynamic-slice_fusion.1) | data formatting | bytes 16777216
  27.1 17.1 %convolution_bitcast_fusion = f32[1024,4,1024]{2,0,1:T(8,128)} fusion(bf16[1024,4,1024]{0,2,1:T(8,128)(2,1)} %bitcast.98), kind=kOutput, calls=%fused_computation | convolution fusion | flops 8589934592 | bytes 25165824 | tf_op jit(solution)/shard_map/tkr,tkc->rkc/dot_general | solution.py:49
  44.5 300.7 %all-reduce.2.cloned.1.call-done = f32[1024,4,1024]{2,0,1:T(8,128)} async-done(((f32[1024,4,1024]{2,0,1:T(8,128)}), f32[1024,4,1024]{2,0,1:T(8,128)}) %all-reduce.2.cloned.1.call-update) | async-done | bytes 16777232 | tf_op jit(solution)/shard_map/psum | solution.py:48
  346.6 31.8 %psum.15 = f32[4]{0:T(128)S(1)} all-reduce(f32[4]{0:T(128)S(1)} %multiply_reduce_fusion), channel_id=1, replica_groups=mesh['dp'=16,'tensor'=2] {'dp'}, use_global_device_ids=true, to_apply=%region_2.3 | all-reduce | flops 4 | bytes 32 | tf_op jit(solution)/shard_map/psum | solution.py:56
  379.0 5.5 pmax.7
  386.3 47.5 %all-gather.11.cloned.1.call-done = f32[1024,1024]{1,0:T(8,128)} async-done(((f32[64,1024]{1,0:T(8,128)}), f32[1024,1024]{1,0:T(8,128)}) %all-gather.11.cloned.1.call-update) | async-done | bytes 4194320 | tf_op jit(solution)/shard_map/all_gather | solution.py:60
  433.8 11.8 %fusion.4 = f32[64,4,1024]{2,0,1:T(8,128)S(1)} fusion(f32[1024,1024]{1,0:T(8,128)} %all-gather.11.cloned.1.call-done, f32[1024,4,1024]{2,0,1:T(8,128)} %all-reduce.2.cloned.1.call-done, s32[]{:T(128)S(6)} %select_n.124, f32[64,1024]{1,0:T(8,128)S(1)} %fusion.18), kind=kOutput, calls=%fused_computation.21 | convolution fusion | flops 3221749760 | bytes 6553604 | tf_op jit(solution)/shard_map/rkj,jkc->rkc/dot_general | solution.py:61
  445.6 12.8 %fusion.10 = f32[64,4,1024]{2,0,1:T(8,128)} fusion(f32[64,4,1024]{2,0,1:T(8,128)S(1)} %fusion.4, f32[1024,1024]{1,0:T(8,128)} %all-gather.11.cloned.1.call-done, f32[64,1024]{1,0:T(8,128)S(1)} %get-tuple-element.5), kind=kOutput, calls=%fused_computation.23 | convolution fusion | flops 3221487616 | bytes 6553600 | tf_op jit(solution)/shard_map/rkj,jkc->rkc/dot_general | solution.py:62
  458.5 125.1 %all-gather.5.cloned.1.call-done = f32[1024,4,1024]{2,0,1:T(8,128)} async-done(((f32[64,4,1024]{2,0,1:T(8,128)}), f32[1024,4,1024]{2,0,1:T(8,128)}) %all-gather.5.cloned.1.call-update) | async-done | bytes 16777232 | tf_op jit(solution)/shard_map/all_gather | solution.py:60
  583.5 15.3 %convolution_bitcast_fusion.6 = f32[64,4,1024]{2,0,1:T(8,128)S(1)} fusion(f32[1024,4,1024]{2,0,1:T(8,128)} %all-gather.5.cloned.1.call-done, f32[1024,4,1024]{2,0,1:T(8,128)} %all-reduce.2.cloned.1.call-done, s32[]{:T(128)S(6)} %select_n.124, f32[64,1024]{1,0:T(8,128)S(1)} %fusion.18), kind=kOutput, calls=%fused_computation.32 | convolution fusion | flops 3221749760 | bytes 19136516 | tf_op jit(solution)/shard_map/rkj,jkc->rkc/dot_general | solution.py:61
  598.8 11.8 %fusion.15 = f32[64,4,1024]{2,0,1:T(8,128)} fusion(f32[1024,4,1024]{2,0,1:T(8,128)S(1)} %copy-done.1, f32[64,4,1024]{2,0,1:T(8,128)S(1)} %convolution_bitcast_fusion.6, f32[64,4,1024]{2,0,1:T(8,128)S(1)} %copy-done.4), kind=kOutput, calls=%fused_computation.31 | convolution fusion | flops 3221749760 | bytes 19922944 | tf_op jit(solution)/shard_map/rkj,jkc->rkc/dot_general | solution.py:62
  610.7 124.7 %all-gather.7.cloned.1.call-done = f32[1024,4,1024]{2,0,1:T(8,128)} async-done(((f32[64,4,1024]{2,0,1:T(8,128)}), f32[1024,4,1024]{2,0,1:T(8,128)}) %all-gather.7.cloned.1.call-update) | async-done | bytes 16777232 | tf_op jit(solution)/shard_map/all_gather | solution.py:60
  735.4 15.0 %convolution_bitcast_fusion.4 = f32[64,4,1024]{2,0,1:T(8,128)S(1)} fusion(f32[1024,4,1024]{2,0,1:T(8,128)} %all-gather.7.cloned.1.call-done, f32[1024,4,1024]{2,0,1:T(8,128)} %all-reduce.2.cloned.1.call-done, s32[]{:T(128)S(6)} %select_n.124, f32[64,1024]{1,0:T(8,128)S(1)} %fusion.18), kind=kOutput, calls=%fused_computation.29 | convolution fusion | flops 3221749760 | bytes 19136516 | tf_op jit(solution)/shard_map/rkj,jkc->rkc/dot_general | solution.py:61
  750.4 11.8 %fusion.14 = f32[64,4,1024]{2,0,1:T(8,128)} fusion(f32[1024,4,1024]{2,0,1:T(8,128)S(1)} %copy-done.2, f32[64,4,1024]{2,0,1:T(8,128)S(1)} %convolution_bitcast_fusion.4, f32[64,4,1024]{2,0,1:T(8,128)S(1)} %copy-done.5), kind=kOutput, calls=%fused_computation.28 | convolution fusion | flops 3221749760 | bytes 19922944 | tf_op jit(solution)/shard_map/rkj,jkc->rkc/dot_general | solution.py:62
  762.6 13.5 %constant_dynamic-slice_fusion = bf16[1,4096,1792]{2,1,0:T(8,128)(2,1)} fusion(bf16[2,4096,1792]{2,1,0:T(8,128)(2,1)} %param.5, s32[]{:T(128)S(6)} %select_n.123), kind=kLoop, calls=%fused_computation.40 | loop fusion | bytes 29360132 | tf_op jit(solution)/shard_map/jit(dynamic_index_in_dim)/dynamic_slice | solution.py:40
  776.0 111.0 %all-gather.9.cloned.1.call-done = f32[1024,4,1024]{2,0,1:T(8,128)} async-done(((f32[64,4,1024]{2,0,1:T(8,128)}), f32[1024,4,1024]{2,0,1:T(8,128)}) %all-gather.9.cloned.1.call-update) | async-done | bytes 16777232 | tf_op jit(solution)/shard_map/all_gather | solution.py:60
  887.1 15.2 %convolution_bitcast_fusion.2 = f32[64,4,1024]{2,0,1:T(8,128)S(1)} fusion(f32[1024,4,1024]{2,0,1:T(8,128)} %all-gather.9.cloned.1.call-done, f32[1024,4,1024]{2,0,1:T(8,128)} %all-reduce.2.cloned.1.call-done, s32[]{:T(128)S(6)} %select_n.124, f32[64,1024]{1,0:T(8,128)S(1)} %fusion.18), kind=kOutput, calls=%fused_computation.26 | convolution fusion | flops 3221749760 | bytes 19136516 | tf_op jit(solution)/shard_map/rkj,jkc->rkc/dot_general | solution.py:61
  902.3 10.8 %fusion.16 = bf16[64,4,1024]{2,0,1:T(8,128)(2,1)S(1)} fusion(f32[1024,4,1024]{2,0,1:T(8,128)S(1)} %copy-done, f32[64,4,1024]{2,0,1:T(8,128)S(1)} %convolution_bitcast_fusion.2, f32[64,4,1024]{2,0,1:T(8,128)S(1)} %copy-done.3), kind=kOutput, calls=%fused_computation.33 | convolution fusion | flops 3222011904 | bytes 19398656 | tf_op jit(solution)/shard_map/rkj,jkc->rkc/dot_general | solution.py:62
  917.8 12.8 %broadcast_in_dim.10 = f32[4,1024,1792]{2,1,0:T(8,128)} broadcast(f32[]{:T(128)} %constant.118.clone.1), dimensions={} | broadcast | bytes 29360132 | tf_op jit(solution)/shard_map/broadcast_in_dim | solution.py:18
  930.6 9.2 convolution_dynamic-update-slice_fusion.15
  944.2 9.0 convolution_dynamic-update-slice_fusion.14
  957.1 4.6 collective-permute-start.5
  1027.1 5.3 collective-permute-done.14
  (78 shorter events, 85.6 us)
Async XLA Ops:
  6.5 338.6 %all-reduce.2.cloned.1.call-start = ((), (), s32[]{:S(2)}) async-start(), calls=%async_computation | async-start | bytes 33554432 | tf_op jit(solution)/shard_map/psum | solution.py:48
  44.3 389.5 %all-gather.11.cloned.1.call-start = ((), (), s32[]{:S(2)}) async-start(), calls=%async_computation.4 | async-start | bytes 4456448 | tf_op jit(solution)/shard_map/all_gather | solution.py:60
  386.0 197.5 %all-gather.5.cloned.1.call-start = ((), (), s32[]{:S(2)}) async-start(), calls=%async_computation.1 | async-start | bytes 17825792 | tf_op jit(solution)/shard_map/all_gather | solution.py:60
  458.4 140.4 %copy-start.4 = (f32[64,4,1024]{2,0,1:T(8,128)S(1)}, f32[64,4,1024]{2,0,1:T(8,128)}, u32[]{:S(2)}) copy-start(f32[64,4,1024]{2,0,1:T(8,128)} %fusion.10) | copy-start | bytes 3145732
  458.4 277.0 %all-gather.7.cloned.1.call-start = ((), (), s32[]{:S(2)}) async-start(), calls=%async_computation.2 | async-start | bytes 17825792 | tf_op jit(solution)/shard_map/all_gather | solution.py:60
  610.6 139.8 %copy-start.5 = (f32[64,4,1024]{2,0,1:T(8,128)S(1)}, f32[64,4,1024]{2,0,1:T(8,128)}, u32[]{:S(2)}) copy-start(f32[64,4,1024]{2,0,1:T(8,128)} %fusion.15) | copy-start | bytes 3145732
  610.7 276.4 %all-gather.9.cloned.1.call-start = ((), (), s32[]{:S(2)}) async-start(), calls=%async_computation.3 | async-start | bytes 17825792 | tf_op jit(solution)/shard_map/all_gather | solution.py:60
  776.0 126.3 %copy-start.3 = (f32[64,4,1024]{2,0,1:T(8,128)S(1)}, f32[64,4,1024]{2,0,1:T(8,128)}, u32[]{:S(2)}) copy-start(f32[64,4,1024]{2,0,1:T(8,128)} %fusion.14) | copy-start | bytes 3145732
  913.1 26.6 %collective-permute-start = (bf16[64,4,1024]{2,0,1:T(8,128)(2,1)S(1)}, bf16[64,4,1024]{2,0,1:T(8,128)(2,1)S(1)}, u32[]{:S(2)}, u32[]{:S(2)}) collective-permute-start(bf16[64,4,1024]{2,0,1:T(8,128)(2,1)S(1)} %fusion.16), channel_id=1, source_target_pairs={{0,2},{2,4},{4,6},{6,8},{8,10},{10,12},{12,14},{14,16},{16,18},{18... | collective-permute-start | bytes 1572872 | tf_op jit(solution)/shard_map/ppermute | solution.py:15
  913.4 26.4 %collective-permute-start.1 = (bf16[64,4,1024]{2,0,1:T(8,128)(2,1)S(1)}, bf16[64,4,1024]{2,0,1:T(8,128)(2,1)S(1)}, u32[]{:S(2)}, u32[]{:S(2)}) collective-permute-start(bf16[64,4,1024]{2,0,1:T(8,128)(2,1)S(1)} %fusion.16), channel_id=1, source_target_pairs={{2,0},{4,2},{6,4},{8,6},{10,8},{12,10},{14,12},{16,14},{18,16},{20... | collective-permute-start | bytes 1572872 | tf_op jit(solution)/shard_map/ppermute | solution.py:15
  930.6 22.7 %slice-start.1 = ((s8[14680064]{0:T(1024)(128)(4,1)}), s8[4194304]{0:T(1024)(128)(4,1)S(1)}, s32[]{:S(2)}) async-start(s8[14680064]{0:T(1024)(128)(4,1)} %bitcast.82), calls=%async_computation.6 | async-start | bytes 8388608
  939.7 17.4 %collective-permute-start.2 = (bf16[64,4,1024]{2,0,1:T(8,128)(2,1)S(1)}, bf16[64,4,1024]{2,0,1:T(8,128)(2,1)S(1)}, u32[]{:S(2)}, u32[]{:S(2)}) collective-permute-start(bf16[64,4,1024]{2,0,1:T(8,128)(2,1)S(1)} %collective-permute-done), channel_id=1, source_target_pairs={{0,2},{2,4},{4,6},{6,8},{8,10},{10,12},{12,14},{14,16},{16,18},{18... | collective-permute-start | bytes 1572872 | tf_op jit(solution)/shard_map/ppermute | solution.py:28
  939.8 17.3 %collective-permute-start.3 = (bf16[64,4,1024]{2,0,1:T(8,128)(2,1)S(1)}, bf16[64,4,1024]{2,0,1:T(8,128)(2,1)S(1)}, u32[]{:S(2)}, u32[]{:S(2)}) collective-permute-start(bf16[64,4,1024]{2,0,1:T(8,128)(2,1)S(1)} %collective-permute-done.1), channel_id=1, source_target_pairs={{2,0},{4,2},{6,4},{8,6},{10,8},{12,10},{14,12},{16,14},{18,16},{20... | collective-permute-start | bytes 1572872 | tf_op jit(solution)/shard_map/ppermute | solution.py:28
  957.1 12.3 %collective-permute-start.4 = (bf16[64,4,1024]{2,0,1:T(8,128)(2,1)S(1)}, bf16[64,4,1024]{2,0,1:T(8,128)(2,1)S(1)}, u32[]{:S(2)}, u32[]{:S(2)}) collective-permute-start(bf16[64,4,1024]{2,0,1:T(8,128)(2,1)S(1)} %collective-permute-done.2), channel_id=1, source_target_pairs={{0,2},{2,4},{4,6},{6,8},{8,10},{10,12},{12,14},{14,16},{16,18},{18... | collective-permute-start | bytes 1572872 | tf_op jit(solution)/shard_map/ppermute | solution.py:28
  957.1 12.3 %collective-permute-start.5 = (bf16[64,4,1024]{2,0,1:T(8,128)(2,1)S(1)}, bf16[64,4,1024]{2,0,1:T(8,128)(2,1)S(1)}, u32[]{:S(2)}, u32[]{:S(2)}) collective-permute-start(bf16[64,4,1024]{2,0,1:T(8,128)(2,1)S(1)} %collective-permute-done.3), channel_id=1, source_target_pairs={{2,0},{4,2},{6,4},{8,6},{10,8},{12,10},{14,12},{16,14},{18,16},{20... | collective-permute-start | bytes 1572872 | tf_op jit(solution)/shard_map/ppermute | solution.py:28
  969.4 12.1 %collective-permute-start.6 = (bf16[64,4,1024]{2,0,1:T(8,128)(2,1)S(1)}, bf16[64,4,1024]{2,0,1:T(8,128)(2,1)S(1)}, u32[]{:S(2)}, u32[]{:S(2)}) collective-permute-start(bf16[64,4,1024]{2,0,1:T(8,128)(2,1)S(1)} %collective-permute-done.4), channel_id=1, source_target_pairs={{0,2},{2,4},{4,6},{6,8},{8,10},{10,12},{12,14},{14,16},{16,18},{18... | collective-permute-start | bytes 1572872 | tf_op jit(solution)/shard_map/ppermute | solution.py:28
  969.4 14.5 %collective-permute-start.7 = (bf16[64,4,1024]{2,0,1:T(8,128)(2,1)S(1)}, bf16[64,4,1024]{2,0,1:T(8,128)(2,1)S(1)}, u32[]{:S(2)}, u32[]{:S(2)}) collective-permute-start(bf16[64,4,1024]{2,0,1:T(8,128)(2,1)S(1)} %collective-permute-done.5), channel_id=1, source_target_pairs={{2,0},{4,2},{6,4},{8,6},{10,8},{12,10},{14,12},{16,14},{18,16},{20... | collective-permute-start | bytes 1572872 | tf_op jit(solution)/shard_map/ppermute | solution.py:28
  981.5 12.3 %collective-permute-start.8 = (bf16[64,4,1024]{2,0,1:T(8,128)(2,1)S(1)}, bf16[64,4,1024]{2,0,1:T(8,128)(2,1)S(1)}, u32[]{:S(2)}, u32[]{:S(2)}) collective-permute-start(bf16[64,4,1024]{2,0,1:T(8,128)(2,1)S(1)} %collective-permute-done.6), channel_id=1, source_target_pairs={{0,2},{2,4},{4,6},{6,8},{8,10},{10,12},{12,14},{14,16},{16,18},{18... | collective-permute-start | bytes 1572872 | tf_op jit(solution)/shard_map/ppermute | solution.py:28
  983.9 10.4 collective-permute-start.9
  993.9 12.1 %collective-permute-start.10 = (bf16[64,4,1024]{2,0,1:T(8,128)(2,1)S(1)}, bf16[64,4,1024]{2,0,1:T(8,128)(2,1)S(1)}, u32[]{:S(2)}, u32[]{:S(2)}) collective-permute-start(bf16[64,4,1024]{2,0,1:T(8,128)(2,1)S(1)} %collective-permute-done.8), channel_id=1, source_target_pairs={{0,2},{2,4},{4,6},{6,8},{8,10},{10,12},{12,14},{14,16},{16,18},{18... | collective-permute-start | bytes 1572872 | tf_op jit(solution)/shard_map/ppermute | solution.py:28
  994.3 13.4 %collective-permute-start.11 = (bf16[64,4,1024]{2,0,1:T(8,128)(2,1)S(1)}, bf16[64,4,1024]{2,0,1:T(8,128)(2,1)S(1)}, u32[]{:S(2)}, u32[]{:S(2)}) collective-permute-start(bf16[64,4,1024]{2,0,1:T(8,128)(2,1)S(1)} %collective-permute-done.9), channel_id=1, source_target_pairs={{2,0},{4,2},{6,4},{8,6},{10,8},{12,10},{14,12},{16,14},{18,16},{20... | collective-permute-start | bytes 1572872 | tf_op jit(solution)/shard_map/ppermute | solution.py:28
  1006.0 13.2 %collective-permute-start.12 = (bf16[64,4,1024]{2,0,1:T(8,128)(2,1)S(1)}, bf16[64,4,1024]{2,0,1:T(8,128)(2,1)S(1)}, u32[]{:S(2)}, u32[]{:S(2)}) collective-permute-start(bf16[64,4,1024]{2,0,1:T(8,128)(2,1)S(1)} %collective-permute-done.10), channel_id=1, source_target_pairs={{0,2},{2,4},{4,6},{6,8},{8,10},{10,12},{12,14},{14,16},{16,18},{18... | collective-permute-start | bytes 1572872 | tf_op jit(solution)/shard_map/ppermute | solution.py:28
  1007.7 15.6 %collective-permute-start.13 = (bf16[64,4,1024]{2,0,1:T(8,128)(2,1)S(1)}, bf16[64,4,1024]{2,0,1:T(8,128)(2,1)S(1)}, u32[]{:S(2)}, u32[]{:S(2)}) collective-permute-start(bf16[64,4,1024]{2,0,1:T(8,128)(2,1)S(1)} %collective-permute-done.11), channel_id=1, source_target_pairs={{2,0},{4,2},{6,4},{8,6},{10,8},{12,10},{14,12},{16,14},{18,16},{20... | collective-permute-start | bytes 1572872 | tf_op jit(solution)/shard_map/ppermute | solution.py:28
  1019.1 13.3 %collective-permute-start.14 = (bf16[64,4,1024]{2,0,1:T(8,128)(2,1)S(1)}, bf16[64,4,1024]{2,0,1:T(8,128)(2,1)S(1)}, u32[]{:S(2)}, u32[]{:S(2)}) collective-permute-start(bf16[64,4,1024]{2,0,1:T(8,128)(2,1)S(1)} %collective-permute-done.12), channel_id=1, source_target_pairs={{0,2},{2,4},{4,6},{6,8},{8,10},{10,12},{12,14},{14,16},{16,18},{18... | collective-permute-start | bytes 1572872 | tf_op jit(solution)/shard_map/ppermute | solution.py:28
  (6 other events, 95.2 us)
Sparse Core Ops, SparseCore 0:
  44.4 300.6 all-reduce.1
  386.2 47.6 all-gather.10
  458.5 124.9 all-gather.4
  610.8 124.6 all-gather.6
  762.4 124.6 all-gather.8
